TPU v7x, 512 devices: a whole 4x4x16 slice. The times are simulated.
512 devices in a mesh: section: 64 (over y_hi, z, core), mp: 8 (over y_lo, x).
Axes of the slice: x: 4, y: 4 (y_hi: 2, y_lo: 2; y = y_hi * 2 + y_lo), z: 16, core: 2. Of those that a mesh axis runs over, the one named last changes fastest.
Arguments:
- gate_weight: bfloat16 [2, 2048, 5632], P(None, 'section', 'mp'), may hold values from -6 to 6
- up_weight: bfloat16 [2, 2048, 5632], P(None, 'section', 'mp'), may hold values from -6 to 6
- hidden_map: int32 [2048], replicated, may hold values from 0 to 2047, as said below
- ffn_map: int32 [5376], replicated, may hold values from 0 to 5631, as said below
Outputs:
- grown_gate: bfloat16 [2, 2, 2048, 11008], P(None, None, 'section', 'mp')
- grown_up: bfloat16 [2, 2, 2048, 11008], P(None, None, 'section', 'mp')
Inputs may be any that keep to these rules, and one draw needn't show every extreme that they name: `hidden_map`: entry i names the old unit copied by new unit 2048 + i. Within each aligned block of 32 entries, at most 1 entries name units of any one block of 32 old units, and some block of old units is named exactly 1 times. `ffn_map`: entry j names the FFN unit of the next layer copied by added unit j % 672 of FFN block j // 672. Within each aligned block of 672 entries, at most 84 entries name units of any one block of 704 old FFN units, and in each aligned block some block of old units is named exactly 84 times.
All inputs are finite; a program needn't handle non-finite values.
Results may differ from a plain program's by a relative error of at most 0.001.
Values may be sent and summed in bfloat16 or wider, within the bound.
A program may use at most 64 MiB of HBM per device.

v0:
```python
import jax
import jax.numpy as jnp
from jax import lax
from jax.sharding import PartitionSpec as P


def sent_together(arrays, axis, split_dim, concat_dim, along):
    ends, at = ([], 0)
    for a in arrays[:-1]:
        at += a.shape[along]
        ends.append(at)
    both = jnp.concatenate(arrays, axis=along)
    return tuple(
        jnp.split(
            lax.all_to_all(both, axis, split_axis=split_dim, concat_axis=concat_dim, tiled=True),
            ends,
            axis=along,
        )
    )


def local(gate_weight, up_weight, hidden_map, ffn_map):
    layers, shard_rows, narrow = gate_weight.shape
    blocks = lax.axis_size("section")
    splits = lax.axis_size("mp")
    section_rank = lax.axis_index("section")
    column_rank = lax.axis_index("mp")
    d_old = shard_rows * blocks
    extra_dev = ffn_map.shape[0] // splits
    wide_cols = narrow + extra_dev
    route_cap = max(1, shard_rows // blocks)
    column_cap = (extra_dev + splits - 1) // splits
    next_pick = jnp.minimum(jnp.arange(layers, dtype=jnp.int32) + 1, layers - 1) - 1
    counts = (
        jax.ops.segment_sum(jnp.ones((d_old,), jnp.float32), hidden_map, num_segments=d_old) + 1.0
    )
    own_rows = section_rank * shard_rows + jnp.arange(shard_rows, dtype=jnp.int32)
    copied = lax.dynamic_slice_in_dim(hidden_map, section_rank * shard_rows, shard_rows)
    mine_extra = lax.dynamic_slice_in_dim(ffn_map, column_rank * extra_dev, extra_dev)
    table = hidden_map.reshape(blocks, shard_rows)
    owner = table // shard_rows
    wanted = owner == section_rank
    order = jnp.cumsum(wanted.astype(jnp.int32), axis=1) - 1
    slot_ids = jnp.arange(route_cap, dtype=jnp.int32)
    selected = wanted[:, None, :] & (order[:, None, :] == slot_ids[None, :, None])
    sent_rows = jnp.sum(jnp.where(selected, (table % shard_rows)[:, None, :], 0), axis=2).reshape(
        -1
    )
    mine_owner = copied // shard_rows
    row_ids = jnp.arange(shard_rows, dtype=jnp.int32)
    earlier = row_ids[None, :] < row_ids[:, None]
    rank_among = jnp.sum(
        (earlier & (mine_owner[None, :] == mine_owner[:, None])).astype(jnp.int32), axis=1
    )
    landing = mine_owner * route_cap + rank_among
    arrived = sent_together(
        (jnp.take(gate_weight, sent_rows, axis=1), jnp.take(up_weight, sent_rows, axis=1)),
        "section",
        1,
        1,
        0,
    )
    doubled_gate = jnp.concatenate([gate_weight, jnp.take(arrived[0], landing, axis=1)], axis=1)
    doubled_up = jnp.concatenate([up_weight, jnp.take(arrived[1], landing, axis=1)], axis=1)
    pair = (doubled_gate, doubled_up)
    later = tuple((portion[1:] for portion in pair))
    column_table = ffn_map.reshape(splits, extra_dev)
    needed = column_table // narrow == column_rank
    rank_cols = jnp.cumsum(needed.astype(jnp.int32), axis=1) - 1
    cap_ids = jnp.arange(column_cap, dtype=jnp.int32)
    picked = needed[:, None, :] & (rank_cols[:, None, :] == cap_ids[None, :, None])
    send_cols = jnp.sum(jnp.where(picked, (column_table % narrow)[:, None, :], 0), axis=2).reshape(
        -1
    )
    outgoing = tuple((jnp.take(portion, send_cols, axis=2) for portion in later))
    arrived = sent_together((outgoing[0], outgoing[1]), "mp", 2, 2, 0)
    extra_owner = mine_extra // narrow
    extra_ids = jnp.arange(extra_dev, dtype=jnp.int32)
    before = extra_ids[None, :] < extra_ids[:, None]
    extra_rank = jnp.sum(
        (before & (extra_owner[None, :] == extra_owner[:, None])).astype(jnp.int32), axis=1
    )
    placed = extra_owner * column_cap + extra_rank
    extras = tuple((jnp.take(portion, placed, axis=2) for portion in arrived))
    wide_gate, wide_up = tuple(
        (
            jnp.concatenate([portion, added[next_pick]], axis=2)
            for portion, added in zip(pair, extras)
        )
    )
    grown_gate = wide_gate.reshape(layers, 2, shard_rows, wide_cols)
    grown_up = wide_up.reshape(layers, 2, shard_rows, wide_cols)
    divisor = jnp.stack([counts[own_rows], counts[copied]])[None, :, :, None]
    return (
        (grown_gate.astype(jnp.float32) / divisor).astype(jnp.bfloat16),
        (grown_up.astype(jnp.float32) / divisor).astype(jnp.bfloat16),
    )


def solution(mesh):
    in_specs = (P(None, "section", "mp"), P(None, "section", "mp"), P(), P())
    out_specs = (P(None, None, "section", "mp"), P(None, None, "section", "mp"))
    return jax.shard_map(local, mesh=mesh, in_specs=in_specs, out_specs=out_specs, check_vma=False)
```

profile of v0, /device:TPU:1, one launch (start us, length us, event | category | flops | bytes accessed | tf_op | source)
XLA Modules:
  0.0 78.9 jit_solution(11409031282616476083)
XLA Ops:
  0.6 0.8 %reshape.313 = s32[64,1,32]{2,0,1:T(8,128)S(1)} reshape(s32[2048]{0:T(1024)} %param.14) | data formatting | bytes 16384 | tf_op jit(solution)/shard_map/reshape | solution.py:40
  1.9 1.2 %gather_fusion.3 = bf16[64,2,704]{2,0,1:T(8,128)(2,1)S(1)} fusion(bf16[2,32,704]{2,1,0:T(8,128)(2,1)S(1)} %copy-done.1, s32[1024]{0:T(1024)S(1)} %pad_clamp_fusion.5), kind=kCustom, calls=%fused_computation.4.clone | custom fusion | bytes 360704 | tf_op jit(solution)/shard_map/jit(_take)/gather | solution.py:57
  3.1 1.2 %gather_fusion.2 = bf16[64,2,704]{2,0,1:T(8,128)(2,1)S(1)} fusion(bf16[2,32,704]{2,1,0:T(8,128)(2,1)S(1)} %copy-done, s32[1024]{0:T(1024)S(1)} %pad_clamp_fusion.5), kind=kCustom, calls=%fused_computation.clone | custom fusion | bytes 360704 | tf_op jit(solution)/shard_map/jit(_take)/gather | solution.py:57
  4.4 1.0 %copy.79 = bf16[4,64,704]{2,0,1:T(4,128)(2,1)} copy(bf16[4,64,704]{2,1,0:T(8,128)(2,1)S(1)} %pad_maximum_fusion) | data formatting | bytes 720896 | tf_op jit(solution)/shard_map/concatenate | solution.py:12
  5.5 19.9 %all-to-all-start = ((bf16[4,64,704]{2,0,1:T(4,128)(2,1)}), bf16[4,64,704]{2,0,1:T(4,128)(2,1)S(1)}, u32[]{:S(2)}, u32[]{:S(2)}) async-start(bf16[4,64,704]{2,0,1:T(4,128)(2,1)} %copy.79), calls=%async_computation | async-start | bytes 786432 | tf_op jit(solution)/shard_map/all_to_all | solution.py:15
  26.1 1.7 %reduce-window.6 = s32[8,6,128]{2,0,1:T(8,128)S(1)} reduce-window(s32[8,6,128]{2,0,1:T(8,128)S(1)} %convert_bitcast_fusion, s32[]{:T(128)} %constant.124.clone.1), window={size=1x1x128 pad=0_0x0_0x127_0}, to_apply=%region_3.6 | reduce-window | flops 780288 | bytes 49156 | tf_op jit(solution)/shard_map/reduce-window
  28.3 1.5 %select_reduce_fusion = s32[8,84]{0,1:T(8,128)S(1)} fusion(s32[8,672]{1,0:T(8,128)S(1)} %add_select_fusion.2, s32[8,672]{1,0:T(8,128)S(1)} %slice_add_fusion, pred[8,672]{1,0:T(8,128)(4,1)S(1)} %fusion.15), kind=kLoop, calls=%fused_computation.13 | loop fusion | flops 1805664 | bytes 51072 | tf_op jit(solution)/shard_map/reduce_sum | solution.py:72
  29.9 11.5 %scatter_fusion = f32[2048]{0:T(1024)S(1)} fusion(f32[2048]{0:T(1024)S(1)} %broadcast_in_dim.80, s32[2048]{0:T(1024)S(1)} %copy-done.3, f32[2048]{0:T(1024)S(1)} %broadcast_in_dim.80), kind=kCustom, calls=%fused_computation.10 | custom fusion | flops 2048 | bytes 32768 | tf_op jit(solution)/shard_map/scatter-add | solution.py:35
  41.4 0.7 gather_fusion.1
  42.1 0.7 gather_fusion
  43.1 0.3 convert_reduce_fusion
  43.6 10.6 %all-to-all-done = bf16[4,64,704]{2,0,1:T(4,128)(2,1)S(1)} async-done(((bf16[4,64,704]{2,0,1:T(4,128)(2,1)}), bf16[4,64,704]{2,0,1:T(4,128)(2,1)S(1)}, u32[]{:S(2)}, u32[]{:S(2)}) %all-to-all-start) | async-done | bytes 360480 | tf_op jit(solution)/shard_map/all_to_all | solution.py:15
  54.2 0.3 fusion.21
  54.5 0.8 gather_fusion.4
  55.3 0.8 gather_fusion.6
  56.5 2.0 %gather_fusion.5 = bf16[672,64]{1,0:T(8,128)(2,1)S(1)} fusion(bf16[64,704]{0,1:T(8,128)(2,1)S(1)} %copy.84, s32[1024]{0:T(1024)S(1)} %pad_clamp_fusion.3), kind=kCustom, calls=%fused_computation.2.clone | custom fusion | bytes 174720 | tf_op jit(solution)/shard_map/jit(_take)/gather | solution.py:75
  58.5 2.0 %gather_fusion.7 = bf16[672,64]{1,0:T(8,128)(2,1)S(1)} fusion(bf16[64,704]{0,1:T(8,128)(2,1)S(1)} %copy.86, s32[1024]{0:T(1024)S(1)} %pad_clamp_fusion.3), kind=kCustom, calls=%fused_computation.6.clone | custom fusion | bytes 174720 | tf_op jit(solution)/shard_map/jit(_take)/gather | solution.py:75
  61.0 0.9 %reshape.452 = bf16[8,2,5376]{2,1,0:T(2,128)(2,1)} reshape(bf16[672,2,64]{2,1,0:T(2,128)(2,1)S(1)} %bitcast.65) | data formatting | bytes 344064
  61.9 4.1 %all-to-all-start.1 = ((bf16[8,2,5376]{2,1,0:T(2,128)(2,1)}), bf16[8,2,5376]{2,1,0:T(2,128)(2,1)S(1)}, u32[]{:S(2)}, u32[]{:S(2)}) async-start(bf16[8,2,5376]{2,1,0:T(2,128)(2,1)} %reshape.452), calls=%async_computation.1 | async-start | bytes 344064 | tf_op jit(solution)/shard_map/all_to_all | solution.py:15
  66.1 6.2 %all-to-all-done.1 = bf16[8,2,5376]{2,1,0:T(2,128)(2,1)S(1)} async-done(((bf16[8,2,5376]{2,1,0:T(2,128)(2,1)}), bf16[8,2,5376]{2,1,0:T(2,128)(2,1)S(1)}, u32[]{:S(2)}, u32[]{:S(2)}) %all-to-all-start.1) | async-done | bytes 172064 | tf_op jit(solution)/shard_map/all_to_all | solution.py:15
  72.5 0.5 fusion.22
  73.1 2.0 %gather_fusion.9 = bf16[672,64]{1,0:T(8,128)(2,1)S(1)} fusion(bf16[64,672]{0,1:T(8,128)(2,1)S(1)} %bitcast.60, s32[1024]{0:T(1024)S(1)} %pad_clamp_fusion.2), kind=kCustom, calls=%fused_computation.7.clone | custom fusion | bytes 174720 | tf_op jit(solution)/shard_map/jit(_take)/gather | solution.py:84
  75.1 2.0 %gather_fusion.8 = bf16[672,64]{1,0:T(8,128)(2,1)S(1)} fusion(bf16[64,672]{0,1:T(8,128)(2,1)S(1)} %bitcast.61, s32[1024]{0:T(1024)S(1)} %pad_clamp_fusion.2), kind=kCustom, calls=%fused_computation.3.clone | custom fusion | bytes 174720 | tf_op jit(solution)/shard_map/jit(_take)/gather | solution.py:84
  77.8 1.1 %fusion.2 = (bf16[2,2,32,1376]{3,2,1,0:T(8,128)(2,1)}, bf16[2,2,32,1376]{3,2,1,0:T(8,128)(2,1)}) fusion(bf16[2,2,32,1376]{3,2,1,0:T(8,128)(2,1)S(1)} %bitcast.64, f32[2,32]{1,0:T(2,128)S(1)} %pad_maximum_fusion.6, bf16[2,2,32,1376]{3,2,1,0:T(8,128)(2,1)S(1)} %bitcast.63), kind=kLoop, calls=%fused_computation.18 | loop fusion | flops 1056768 | bytes 1409280 | tf_op jit(solution)/shard_map/convert_element_type | solution.py:96
  (64 shorter events, 4.0 us)
Async XLA Ops:
  0.6 1.2 %copy-start.1 = (bf16[2,32,704]{2,1,0:T(8,128)(2,1)S(1)}, bf16[2,32,704]{2,1,0:T(8,128)(2,1)}, u32[]{:S(2)}) copy-start(bf16[2,32,704]{2,1,0:T(8,128)(2,1)} %param.13) | copy-start | bytes 270340
  1.9 1.2 %copy-start = (bf16[2,32,704]{2,1,0:T(8,128)(2,1)S(1)}, bf16[2,32,704]{2,1,0:T(8,128)(2,1)}, u32[]{:S(2)}) copy-start(bf16[2,32,704]{2,1,0:T(8,128)(2,1)} %param.12) | copy-start | bytes 270340
  5.5 19.9 %copy-start.2 = (s32[5376]{0:T(1024)S(1)}, s32[5376]{0:T(1024)}, u32[]{:S(2)}) copy-start(s32[5376]{0:T(1024)} %param.15) | copy-start | bytes 64516
  5.5 20.0 %copy-start.3 = (s32[2048]{0:T(1024)S(1)}, s32[2048]{0:T(1024)}, u32[]{:S(2)}) copy-start(s32[2048]{0:T(1024)} %param.14) | copy-start | bytes 24580
  5.5 48.7 %all-to-all-start = ((bf16[4,64,704]{2,0,1:T(4,128)(2,1)}), bf16[4,64,704]{2,0,1:T(4,128)(2,1)S(1)}, u32[]{:S(2)}, u32[]{:S(2)}) async-start(bf16[4,64,704]{2,0,1:T(4,128)(2,1)} %copy.79), calls=%async_computation | async-start | bytes 786432 | tf_op jit(solution)/shard_map/all_to_all | solution.py:15
  61.9 10.3 %all-to-all-start.1 = ((bf16[8,2,5376]{2,1,0:T(2,128)(2,1)}), bf16[8,2,5376]{2,1,0:T(2,128)(2,1)S(1)}, u32[]{:S(2)}, u32[]{:S(2)}) async-start(bf16[8,2,5376]{2,1,0:T(2,128)(2,1)} %reshape.452), calls=%async_computation.1 | async-start | bytes 344064 | tf_op jit(solution)/shard_map/all_to_all | solution.py:15
where the time goes:
time: 79.2 us; the launch traced here: 78.9 us
  starting transfers between devices  24 us (30%)
  local copies, waits for them, and re-layouts  18.7 us (24%)
  other arithmetic  18.3 us (23%)
  waiting for transfers between devices  16.8 us (21%)
  between operations  1.04 us (1%)
    all_to_all x2, starting transfers between devices, sent_together(): lax.all_to_all(both, axis, split_axis=split_dim, concat_axis=concat_dim,...  24 us
    all_to_all x2, waiting for transfers between devices, sent_together(): lax.all_to_all(both, axis, split_axis=split_dim, concat_axis=concat_dim,...  16.8 us
    scatter-add x1, other arithmetic, local(): jax.ops.segment_sum(jnp.ones((d_old,), jnp.float32), hidden_map, num_segm...  11.5 us
    gather x2, local copies, waits for them, and re-layouts, local(): jnp.take(portion, send_cols, axis=2)  4.01 us
    gather x2, local copies, waits for them, and re-layouts, local(): extras = tuple((jnp.take(portion, placed, axis=2) for portion in arrived))  4.01 us
    another operation x4, other arithmetic  1.95 us
  transfers between devices with their start and end apart: 2, of which 2 were waited for; matrix products, arithmetic and copies ran while one was open for 23% of the time, Pallas kernels for 0%

commit v1 on v0

v1 whole, which is shorter than its diff:
```python
import jax
import jax.numpy as jnp
from jax import lax
from jax.experimental import pallas as pl
from jax.experimental.pallas import tpu as pltpu
from jax.sharding import PartitionSpec as P

MESH = pl.DeviceIdType.MESH
BF16, F32, I32 = jnp.bfloat16, jnp.float32, jnp.int32
LANES = 128


def lane_iota(shape):
    return lax.broadcasted_iota(I32, shape, len(shape) - 1)


def row_iota(shape):
    return lax.broadcasted_iota(I32, shape, len(shape) - 2)


def ranks(hit, wide):
    upper = row_iota((LANES, LANES)) < lane_iota((LANES, LANES))
    steps = jnp.concatenate([upper.astype(F32), jnp.ones((LANES, LANES), F32)], axis=1).astype(BF16)
    flags = hit.astype(F32).astype(BF16)
    carry = jnp.zeros((hit.shape[0], LANES), F32)
    pieces = []
    for t in range(wide // LANES):
        both = jnp.dot(flags[:, t * LANES : (t + 1) * LANES], steps, preferred_element_type=F32)
        pieces.append(both[:, :LANES] + carry)
        carry = carry + both[:, LANES:]
    return jnp.concatenate(pieces, axis=1).astype(I32)


def solution(mesh):
    blocks, splits = mesh.shape["section"], mesh.shape["mp"]

    def local(gate_weight, up_weight, hidden_map, ffn_map):
        layers, rows, narrow = gate_weight.shape
        extra = ffn_map.shape[0] // splits
        wide = narrow + extra
        cap = extra // splits
        slots = -(-cap // 32) * 32
        main = narrow // LANES * LANES
        tail = narrow - main
        lead = main + LANES
        spread = -(-(wide - main) // LANES) * LANES
        hrows = hidden_map.shape[0] // LANES
        frows = ffn_map.shape[0] // LANES
        per_row = LANES // rows
        z_chips = blocks // 4

        def kernel(gate_h, up_h, hmap_h, fmap_h, out_g, out_u, gv, uv, hm, fm, own1, own0, send1, recv1, send0, recv0,
                   xs, fr, colpick, place, bsend, brecv, stage, in_sem, s1, r1, s0, r0, sb, rb, out_sem):
            me = lax.axis_index("section")
            col = lax.axis_index("mp")
            half, z, core = me // (2 * z_chips), (me // 2) % z_chips, me % 2

            def peer(i):
                n = i // 4
                step = (n + 1) // 2
                dz = z_chips // 2 + jnp.where(n % 2 == 1, -step, step)
                other = 3 - i % 4
                return ((half + other // 2) % 2) * (2 * z_chips) + ((z + dz) % z_chips) * 2 + (core + other % 2) % 2

            barrier = pltpu.get_barrier_semaphore()

            @pl.loop(0, blocks - 1)
            def _(i):
                pl.semaphore_signal(barrier, 1, device_id={"section": peer(i)}, device_id_type=MESH)

            for k in range(1, splits):
                pl.semaphore_signal(barrier, 1, device_id={"mp": (col + k) % splits}, device_id_type=MESH)

            loads = [
                pltpu.make_async_copy(src, dst, in_sem.at[n])
                for n, (src, dst) in enumerate(((hmap_h, hm), (gate_h, gv), (up_h, uv), (fmap_h, fm)))
            ]
            for copy in loads:
                copy.start()

            loads[0].wait()
            spread_map = jnp.concatenate([jnp.broadcast_to(hm[r : r + 1, :], (2 * per_row, LANES)) for r in range(hrows)], axis=0)
            shape = (2 * blocks, LANES)
            within = spread_map - me * rows
            mine = (within >= 0) & (within < rows) & (lane_iota(shape) // rows == (row_iota(shape) // 2) % per_row)
            chosen = jnp.sum(jnp.where(mine, within + 1, 0), axis=1, keepdims=True) - 1
            side = row_iota((2 * blocks, 1)) % 2
            target = jnp.where(chosen >= 0, chosen + side * rows, -1)
            pick_rows = (target == lane_iota((2 * blocks, 2 * rows))).astype(F32).astype(BF16)

            used = jnp.zeros((rows, LANES), F32)
            for r in range(hrows):
                entry = jnp.broadcast_to(hm[r : r + 1, :], (rows, LANES))
                used = used + (entry == me * rows + row_iota((rows, LANES))).astype(F32)
            counts = jnp.sum(used, axis=1, keepdims=True) + 1.0
            counts = jnp.concatenate([counts, counts], axis=0)

            loads[1].wait()
            loads[2].wait()
            new = [
                (jnp.concatenate([gv[layer], uv[layer]], axis=0).astype(F32) / counts) for layer in range(2)
            ]
            own1[:, :main] = new[1][:, :main].astype(BF16)
            own1[:, main:] = jnp.concatenate([new[1][:, main:], new[0][:, main:]], axis=1).astype(BF16)
            own0[...] = new[0][:, :main].astype(BF16)
            send1[...] = jnp.dot(pick_rows, own1[...], preferred_element_type=F32).astype(BF16).reshape(send1.shape)
            send0[...] = jnp.dot(pick_rows, own0[...], preferred_element_type=F32).astype(BF16).reshape(send0.shape)

            pl.semaphore_wait(barrier, blocks + splits - 2)

            for src, dst, ss, rs in ((send1, recv1, s1, r1), (send0, recv0, s0, r0)):

                @pl.loop(0, blocks - 1)
                def _(i, src=src, dst=dst, ss=ss, rs=rs):
                    to = peer(i)
                    pltpu.make_async_remote_copy(
                        src.at[to], dst.at[me], ss, rs, device_id={"section": to}, device_id_type=MESH
                    ).start()

            recv1[me] = send1[me]
            recv0[me] = send0[me]

            entry = jnp.broadcast_to(hm[pl.ds(me // per_row, 1), :], (rows, LANES))
            place_of = lane_iota((rows, LANES)) == (me % per_row) * rows + row_iota((rows, LANES))
            owner = jnp.sum(jnp.where(place_of, entry, 0), axis=1, keepdims=True) // rows
            landing = jnp.concatenate([2 * owner, 2 * owner + 1], axis=0)
            arrive = (landing == lane_iota((2 * rows, 2 * blocks))).astype(F32).astype(BF16)

            loads[3].wait()
            padded = -(-extra // LANES) * LANES
            for m in range(splits):
                first, shift = m * extra // LANES, m * extra % LANES
                n_rows = min(padded // LANES + 1, frows - first)
                flat = jnp.concatenate([fm[first + r : first + r + 1, :] for r in range(n_rows)], axis=1)
                flat = flat[:, shift : shift + extra]
                fr[m : m + 1, :extra] = flat
            fr[:, extra:] = jnp.full((splits, fr.shape[1] - extra), -1, I32)

            named = fr[...]
            within = named - col * narrow
            hit = (within >= 0) & (within < narrow)
            rank = jnp.where(hit, ranks(hit, padded), -1)
            for m in range(splits):
                taken = rank[m : m + 1, :] == row_iota((slots, padded))
                column = jnp.sum(jnp.where(taken, within[m : m + 1, :] + 1, 0), axis=1, keepdims=True) - 1
                colpick[m * slots : (m + 1) * slots, :] = (column == lane_iota((slots, narrow))).astype(F32).astype(BF16)

            wanted = jnp.broadcast_to(fr[pl.ds(col, 1), :], (splits, padded)) - row_iota((splits, padded)) * narrow
            hit = (wanted >= 0) & (wanted < narrow)
            code = jnp.where(hit, ranks(hit, padded) + row_iota((splits, padded)) * slots + 1, 0)
            code = jnp.sum(code, axis=0, keepdims=True) - 1
            code = jnp.concatenate([jnp.full((1, tail), -1, I32), code[:, : spread - tail]], axis=1)
            place[...] = (code == row_iota((splits * slots, spread))).astype(F32).astype(BF16)

            pltpu.make_async_copy(send1.at[pl.ds(0, blocks - 1)], recv1.at[pl.ds(0, blocks - 1)], r1).wait()
            got1 = jnp.dot(arrive, recv1[...].reshape(2 * blocks, lead), preferred_element_type=F32).astype(BF16)
            for w in range(2):
                a, b = w * rows, (w + 1) * rows
                xs[2 * a : 2 * a + rows, :] = own1[a:b, :]
                xs[2 * a + rows : 2 * b, :] = got1[a:b, :]
            bsend[...] = (
                lax.dot_general(colpick[...], xs[:, :narrow], (((1,), (1,)), ((), ())), preferred_element_type=F32)
                .astype(BF16)
                .reshape(bsend.shape)
            )
            for k in range(1, splits):
                to = (col + k) % splits
                pltpu.make_async_remote_copy(
                    bsend.at[to], brecv.at[col], sb, rb, device_id={"mp": to}, device_id_type=MESH
                ).start()
            brecv[col] = bsend[col]

            last = xs[:, main:].astype(F32)
            first_half = lane_iota((4 * rows, LANES)) < tail
            pads = [jnp.zeros((4 * rows, spread - LANES), F32)]
            ends = [jnp.where(first_half, end, 0.0) for end in (pltpu.roll(last, LANES - tail, 1), last)]
            for w in range(2):
                for k in range(2):
                    a = (2 * w + k) * rows
                    stage[w, 1, k, :, :main] = xs[a : a + rows, :main]
                stage[w, 0, 0, :, :main] = own0[w * rows : (w + 1) * rows, :]

            pltpu.make_async_copy(bsend.at[pl.ds(0, splits - 1)], brecv.at[pl.ds(0, splits - 1)], rb).wait()
            added = lax.dot_general(
                brecv[...].reshape(splits * slots, 4 * rows), place[...], (((0,), (0,)), ((), ())), preferred_element_type=F32
            )
            for layer in range(2):
                full = (added + jnp.concatenate([ends[layer]] + pads, axis=1)).astype(BF16)
                for w in range(2):
                    for k in range(2):
                        a = (2 * w + k) * rows
                        stage[w, layer, k, :, main:] = full[a : a + rows, : wide - main]
            outs = (out_g, out_u)
            writes = []
            for w in range(2):
                writes.append(pltpu.make_async_copy(stage.at[w, 1], outs[w].at[1], out_sem.at[3 * w]))
                writes.append(pltpu.make_async_copy(stage.at[w, 0, 0], outs[w].at[0, 0], out_sem.at[3 * w + 1]))
            for copy in writes:
                copy.start()

            pltpu.make_async_copy(send0.at[pl.ds(0, blocks - 1)], recv0.at[pl.ds(0, blocks - 1)], r0).wait()
            got0 = jnp.dot(arrive, recv0[...].reshape(2 * blocks, main), preferred_element_type=F32).astype(BF16)
            for w in range(2):
                stage[w, 0, 1, :, :main] = got0[w * rows : (w + 1) * rows, :]
                copy = pltpu.make_async_copy(stage.at[w, 0, 1], outs[w].at[0, 1], out_sem.at[3 * w + 2])
                copy.start()
                writes.append(copy)
            pltpu.make_async_copy(send1.at[pl.ds(0, blocks - 1)], recv1.at[pl.ds(0, blocks - 1)], s1).wait()
            pltpu.make_async_copy(send0.at[pl.ds(0, blocks - 1)], recv0.at[pl.ds(0, blocks - 1)], s0).wait()
            pltpu.make_async_copy(bsend.at[pl.ds(0, splits - 1)], brecv.at[pl.ds(0, splits - 1)], sb).wait()
            for copy in writes:
                copy.wait()

        padded = -(-extra // LANES) * LANES
        out = jax.ShapeDtypeStruct((layers, 2, rows, wide), BF16)
        anywhere = pl.BlockSpec(memory_space=pl.ANY)
        return pl.pallas_call(
            kernel,
            out_shape=(out, out),
            in_specs=[anywhere] * 4,
            out_specs=(anywhere, anywhere),
            scratch_shapes=[
                pltpu.VMEM(gate_weight.shape, BF16),
                pltpu.VMEM(gate_weight.shape, BF16),
                pltpu.VMEM((hrows, LANES), I32),
                pltpu.VMEM((frows, LANES), I32),
                pltpu.VMEM((2 * rows, lead), BF16),
                pltpu.VMEM((2 * rows, main), BF16),
                pltpu.VMEM((blocks, 2, lead), BF16),
                pltpu.VMEM((blocks, 2, lead), BF16),
                pltpu.VMEM((blocks, 2, main), BF16),
                pltpu.VMEM((blocks, 2, main), BF16),
                pltpu.VMEM((4 * rows, lead), BF16),
                pltpu.VMEM((splits, padded), I32),
                pltpu.VMEM((splits * slots, narrow), BF16),
                pltpu.VMEM((splits * slots, spread), BF16),
                pltpu.VMEM((splits, slots, 4 * rows), BF16),
                pltpu.VMEM((splits, slots, 4 * rows), BF16),
                pltpu.VMEM((2, layers, 2, rows, wide), BF16),
                pltpu.SemaphoreType.DMA((4,)),
                pltpu.SemaphoreType.DMA,
                pltpu.SemaphoreType.DMA,
                pltpu.SemaphoreType.DMA,
                pltpu.SemaphoreType.DMA,
                pltpu.SemaphoreType.DMA,
                pltpu.SemaphoreType.DMA,
                pltpu.SemaphoreType.DMA((6,)),
            ],
            compiler_params=pltpu.CompilerParams(collective_id=0, has_side_effects=True),
            name="grow",
        )(gate_weight, up_weight, hidden_map.reshape(hrows, LANES), ffn_map.reshape(frows, LANES))

    weights = P(None, "section", "mp")
    out_specs = (P(None, None, "section", "mp"),) * 2
    return jax.shard_map(local, mesh=mesh, in_specs=(weights, weights, P(), P()), out_specs=out_specs, check_vma=False)
```

time: 79.2 us -> 41.4 us (0.52)
  Pallas kernels: 0 us -> 38.1 us
  starting transfers between devices: 24 us -> 0 us
  other arithmetic: 18.3 us -> 0 us
  waiting for transfers between devices: 16.8 us -> 0 us
  local copies, waits for them, and re-layouts: 18.7 us -> 2.53 us
    pallas_call x0 -> x1, Pallas kernels: none -> 38.1 us  [local(): pl.pallas_call(kernel, out_shape=(out, out), in_specs=[anywhere] * 4, out...]
    all_to_all x2 -> x0, starting transfers between devices: 24 us -> none  [sent_together(): lax.all_to_all(both, axis, split_axis=split_dim, concat_axis=concat_dim,...]
    all_to_all x2 -> x0, waiting for transfers between devices: 16.8 us -> none  [sent_together(): lax.all_to_all(both, axis, split_axis=split_dim, concat_axis=concat_dim,...]
    gather x14 -> x0, local copies, waits for them, and re-layouts: 13.6 us -> none  [the longest x2 4.01 us: local(): jnp.take(portion, send_cols, axis=2)]
    scatter-add x1 -> x0, other arithmetic: 11.5 us -> none  [local(): jax.ops.segment_sum(jnp.ones((d_old,), jnp.float32), hidden_map, num_segm...]
    another operation x8 -> x0, other arithmetic: 2.18 us -> none
    reduce_sum x4 -> x0, other arithmetic: 2.17 us -> none  [the longest x1 1.51 us: local(): jnp.sum(jnp.where(picked, (column_table % narrow)[:, None, :], 0), axis=2)]
    unnamed x12 -> x4, local copies, waits for them, and re-layouts: 1.22 us -> 2.53 us
  transfers between devices with their start and end apart: 2 -> 0, of which waited for: 2 -> 0; matrix products, arithmetic and copies ran while one was open for 23% -> 0% of each run, Pallas kernels for 0% -> 0%
where the time goes in v1:
time: 41.4 us; the launch traced here: 41.2 us
  Pallas kernels  38.1 us (92%)
  local copies, waits for them, and re-layouts  2.53 us (6%)
  between operations  0.65 us (2%)
    pallas_call x1, Pallas kernels, local(): pl.pallas_call(kernel, out_shape=(out, out), in_specs=[anywhere] * 4, out...  38.1 us
    unnamed x4, local copies, waits for them, and re-layouts  2.53 us

profile of v1, /device:TPU:1, one launch (start us, length us, event | category | flops | bytes accessed | tf_op | source)
XLA Modules:
  0.0 41.2 jit_solution(17206252766940624365)
XLA Ops:
  0.6 38.1 %grow.1 = (bf16[2,2,32,1376]{3,2,1,0:T(8,128)(2,1)}, bf16[2,2,32,1376]{3,2,1,0:T(8,128)(2,1)}) custom-call(bf16[2,32,704]{2,1,0:T(8,128)(2,1)} %gate_h.1, bf16[2,32,704]{2,1,0:T(8,128)(2,1)} %up_h.1, s32[16,128]{1,0:T(8,128)} %bitcast.3, s32[42,128]{1,0:T(8,128)} %bitcast.2), custom_call_target="tpu_custom_call" | custom-call | tf_op jit(solution)/shard_map/grow/pallas_call | solution.py:217
  38.7 0.0 copy-start
  38.7 1.8 %copy.8 = bf16[2,2,32,1376]{3,2,1,0:T(8,128)(2,1)} copy(bf16[2,2,32,1376]{3,2,1,0:T(8,128)(2,1)} %get-tuple-element.4) | data formatting | bytes 704512
  40.5 0.0 copy-done
  40.5 0.7 %copy.9 = bf16[2,2,32,1376]{3,2,1,0:T(8,128)(2,1)} copy(bf16[2,2,32,1376]{3,2,1,0:T(8,128)(2,1)S(1)} %copy-done) | data formatting | bytes 704512
Async XLA Ops:
  38.7 1.8 %copy-start = (bf16[2,2,32,1376]{3,2,1,0:T(8,128)(2,1)S(1)}, bf16[2,2,32,1376]{3,2,1,0:T(8,128)(2,1)}, u32[]{:S(2)}) copy-start(bf16[2,2,32,1376]{3,2,1,0:T(8,128)(2,1)} %get-tuple-element.5) | copy-start | bytes 1056772

commit v2 on v1

v2 whole, which is shorter than its diff:
```python
import functools

import jax
import jax.numpy as jnp
from jax import lax
from jax.experimental import pallas as pl
from jax.experimental.pallas import tpu as pltpu
from jax.sharding import PartitionSpec as P

MESH = pl.DeviceIdType.MESH
BF16, F32, I32 = jnp.bfloat16, jnp.float32, jnp.int32
LANES = 128


def lane_iota(shape):
    return lax.broadcasted_iota(I32, shape, len(shape) - 1)


def row_iota(shape):
    return lax.broadcasted_iota(I32, shape, len(shape) - 2)


def one_hot(hit):
    return hit.astype(F32).astype(BF16)


def ranks(hit, wide):
    upper = row_iota((LANES, LANES)) < lane_iota((LANES, LANES))
    steps = jnp.concatenate([upper.astype(F32), jnp.ones((LANES, LANES), F32)], axis=1).astype(BF16)
    flags = one_hot(hit)
    carry = jnp.zeros((hit.shape[0], LANES), F32)
    pieces = []
    for t in range(wide // LANES):
        both = jnp.dot(flags[:, t * LANES : (t + 1) * LANES], steps, preferred_element_type=F32)
        pieces.append(both[:, :LANES] + carry)
        carry = carry + both[:, LANES:]
    return jnp.concatenate(pieces, axis=1).astype(I32)


def write_out(gate_v, up_v, gate_h, up_h, sems):
    copies = [
        pltpu.make_async_copy(src.at[layer], dst.at[layer], sems.at[2 * n + layer])
        for n, (src, dst) in enumerate(((gate_v, gate_h), (up_v, up_h)))
        for layer in range(2)
    ]
    for copy in copies:
        copy.start()
    for copy in copies:
        copy.wait()


def solution(mesh):
    blocks, splits = mesh.shape["section"], mesh.shape["mp"]
    z_chips = blocks // 4
    reach = z_chips // 4

    def steps(first, last):
        order = [d for n in range(last, first - 1, -1) for d in ((n, z_chips - n) if 0 < n < z_chips // 2 else (n,))]
        return [(d, q) for d in order for q in range(4) if d or q]

    near = steps(0, reach)
    n_far = z_chips - 2 * reach - 1

    def local(gate_weight, up_weight, hidden_map, ffn_map):
        layers, rows, narrow = gate_weight.shape
        extra = ffn_map.shape[0] // splits
        wide = narrow + extra
        cap = extra // splits
        filled = -(-cap // 32) * 32
        main = narrow // LANES * LANES
        tail = narrow - main
        lead = main + LANES
        padded = -(-extra // LANES) * LANES
        spread = -(-(wide - main) // LANES) * LANES
        hrows = hidden_map.shape[0] // LANES
        frows = ffn_map.shape[0] // LANES
        per_row = LANES // rows
        cols = splits * LANES

        def kernel(gate_h, up_h, hmap_h, fmap_h, out_g, out_u, gv, uv, hm, fm, own1, own0, send1, recv1, send0, recv0,
                   got, fr, colpick, place, bsend, brecv, in_sem, s1, r1, s0, r0, sb, rb, ready):
            outs = (out_g, out_u)
            me = lax.axis_index("section")
            col = lax.axis_index("mp")
            half, z, core = me // (2 * z_chips), (me // 2) % z_chips, me % 2
            ring = [2 * z] + [2 * jnp.where(z + d >= z_chips, z + d - z_chips, z + d) for d in range(1, z_chips)]
            seat = [h * (2 * z_chips) + c for h in (half, 1 - half) for c in (core, 1 - core)]
            fellow = [jnp.where(col + k >= splits, col + k - splits, col + k) for k in range(splits)]

            barrier = pltpu.get_barrier_semaphore()
            for d, q in near:
                pl.semaphore_signal(barrier, 1, device_id={"section": seat[q] + ring[d]}, device_id_type=MESH)
            for to in fellow[1:]:
                pl.semaphore_signal(barrier, 1, device_id={"mp": to}, device_id_type=MESH)

            loads = [
                pltpu.make_async_copy(src, dst, in_sem.at[n])
                for n, (src, dst) in enumerate(((hmap_h, hm), (gate_h, gv), (up_h, uv), (fmap_h, fm)))
            ]
            for copy in loads:
                copy.start()

            loads[0].wait()
            spread_map = jnp.concatenate([jnp.broadcast_to(hm[r : r + 1, :], (2 * per_row, LANES)) for r in range(hrows)], axis=0)
            shape = (2 * blocks, LANES)
            within = spread_map - me * rows
            mine = (within >= 0) & (within < rows) & (lane_iota(shape) // rows == (row_iota(shape) // 2) % per_row)
            chosen = jnp.sum(jnp.where(mine, within + 1, 0), axis=1, keepdims=True) - 1
            side = row_iota((2 * blocks, 1)) % 2
            target = jnp.where(chosen >= 0, chosen + side * rows, -1)
            pick_rows = one_hot(target == lane_iota((2 * blocks, 2 * rows)))

            used = jnp.zeros((rows, LANES), F32)
            for r in range(hrows):
                entry = jnp.broadcast_to(hm[r : r + 1, :], (rows, LANES))
                used = used + (entry == me * rows + row_iota((rows, LANES))).astype(F32)
            counts = jnp.sum(used, axis=1, keepdims=True) + 1.0
            counts = jnp.concatenate([counts, counts], axis=0)

            loads[1].wait()
            loads[2].wait()
            new = [(jnp.concatenate([gv[layer], uv[layer]], axis=0).astype(F32) / counts) for layer in range(2)]
            own1[:, :main] = new[1][:, :main].astype(BF16)
            own1[:, main:] = jnp.concatenate([new[1][:, main:], new[0][:, main:]], axis=1).astype(BF16)
            own0[...] = new[0][:, :main].astype(BF16)
            send1[...] = jnp.dot(pick_rows, own1[...], preferred_element_type=F32).astype(BF16).reshape(send1.shape)
            send0[...] = jnp.dot(pick_rows, own0[...], preferred_element_type=F32).astype(BF16).reshape(send0.shape)
            recv1[me] = send1[me]
            recv0[me] = send0[me]

            pl.semaphore_wait(barrier, len(near) + splits - 1)
            for d in (reach, z_chips - reach):
                pl.semaphore_signal(ready, 1, device_id={"section": seat[0] + ring[d]}, device_id_type=MESH)

            def send(layer, to):
                src, dst, ss, rs = ((send0, recv0, s0, r0), (send1, recv1, s1, r1))[layer]
                pltpu.make_async_remote_copy(
                    src.at[to], dst.at[me], ss, rs, device_id={"section": to}, device_id_type=MESH
                ).start()

            for d, q in near:
                send(1, seat[q] + ring[d])

            loads[3].wait()
            for m in range(splits):
                first, shift = m * extra // LANES, m * extra % LANES
                n_rows = min(padded // LANES + 1, frows - first)
                flat = jnp.concatenate([fm[first + r : first + r + 1, :] for r in range(n_rows)], axis=1)
                fr[m : m + 1, :extra] = flat[:, shift : shift + extra]
            fr[:, extra:] = jnp.full((splits, padded - extra), -1, I32)

            within = fr[...] - col * narrow
            hit = (within >= 0) & (within < narrow)
            rank = jnp.where(hit, ranks(hit, padded), -1)
            for m in range(splits):
                taken = rank[m : m + 1, :] == row_iota((filled, padded))
                column = jnp.sum(jnp.where(taken, within[m : m + 1, :] + 1, 0), axis=1, keepdims=True) - 1
                colpick[m * LANES : m * LANES + filled, :] = one_hot(column == lane_iota((filled, narrow)))
                colpick[m * LANES + filled : (m + 1) * LANES, :] = jnp.zeros((LANES - filled, narrow), BF16)

            def exchange(part, values):
                chosen = lax.dot_general(values, colpick[...], (((1,), (1,)), ((), ())), preferred_element_type=F32).astype(BF16)
                for m in range(splits):
                    bsend[part, m] = chosen[:, m * LANES : (m + 1) * LANES]
                for to in fellow[1:]:
                    pltpu.make_async_remote_copy(
                        bsend.at[part, to], brecv.at[part, col], sb.at[part], rb.at[part], device_id={"mp": to}, device_id_type=MESH
                    ).start()
                brecv[part, col] = bsend[part, col]

            def arrived(buffers, sem):
                src, dst = buffers
                pltpu.make_async_copy(src.at[pl.ds(0, dst.shape[0] - 1)], dst.at[pl.ds(0, dst.shape[0] - 1)], sem).wait()

            def grow(part, last):
                arrived((bsend.at[part], brecv.at[part]), rb.at[part])
                added = jnp.zeros((2 * rows, spread), F32)
                for m in range(splits):
                    added += jnp.dot(brecv[part, m], place[m * LANES : (m + 1) * LANES, :], preferred_element_type=F32)
                first_half = lane_iota((2 * rows, LANES)) < tail
                for layer, end in enumerate((pltpu.roll(last, LANES - tail, 1), last)):
                    head = (added[:, :LANES] + jnp.where(first_half, end, 0.0)).astype(BF16)
                    for w in range(2):
                        a, b = w * rows, (w + 1) * rows
                        outs[w][layer, part, :, main:lead] = head[a:b, :]
                        outs[w][layer, part, :, lead:] = added[a:b, LANES : wide - main].astype(BF16)

            exchange(0, own1[:, :narrow])

            pl.semaphore_wait(ready, 2)
            turned = jnp.where((z + reach + 1 < z_chips) & (z + reach + n_far >= z_chips), z_chips - 1 - reach - z, 0)
            for i in range(n_far):
                ahead = jnp.where(i + turned >= n_far, i + turned - n_far, i + turned) + reach + 1 + z
                for q in range(4):
                    send(1, seat[q] + 2 * jnp.where(ahead >= z_chips, ahead - z_chips, ahead))

            wanted = jnp.broadcast_to(fr[pl.ds(col, 1), :], (splits, padded)) - row_iota((splits, padded)) * narrow
            hit = (wanted >= 0) & (wanted < narrow)
            code = jnp.where(hit, ranks(hit, padded) + row_iota((splits, padded)) * LANES + 1, 0)
            code = jnp.sum(code, axis=0, keepdims=True) - 1
            code = jnp.concatenate([jnp.full((1, tail), -1, I32), code[:, : spread - tail]], axis=1)
            place[...] = one_hot(code == row_iota((cols, spread)))

            entry = jnp.broadcast_to(hm[pl.ds(me // per_row, 1), :], (rows, LANES))
            place_of = lane_iota((rows, LANES)) == (me % per_row) * rows + row_iota((rows, LANES))
            owner = jnp.sum(jnp.where(place_of, entry, 0), axis=1, keepdims=True) // rows
            landing = jnp.concatenate([2 * owner, 2 * owner + 1], axis=0)
            arrive = one_hot(landing == lane_iota((2 * rows, 2 * blocks)))

            for w in range(2):
                a, b = w * rows, (w + 1) * rows
                outs[w][0, 0, :, :main] = own0[a:b, :]
                outs[w][1, 0, :, :main] = own1[a:b, :main]
            arrived((send1, recv1), s1)
            for j in range(z_chips):
                for q in range(1, 4):
                    send(0, seat[q] + 2 * j)
                pl.when(z != j)(functools.partial(send, 0, seat[0] + 2 * j))
            grow(0, own1[:, main:].astype(F32))

            arrived((send1, recv1), r1)
            got[...] = jnp.dot(arrive, recv1[...].reshape(2 * blocks, lead), preferred_element_type=F32).astype(BF16)
            exchange(1, got[:, :narrow])
            for w in range(2):
                outs[w][1, 1, :, :main] = got[w * rows : (w + 1) * rows, :main]
            arrived((send0, recv0), r0)
            got0 = jnp.dot(arrive, recv0[...].reshape(2 * blocks, main), preferred_element_type=F32).astype(BF16)
            for w in range(2):
                outs[w][0, 1, :, :main] = got0[w * rows : (w + 1) * rows, :]
            grow(1, got[:, main:].astype(F32))

            arrived((send0, recv0), s0)
            for part in range(2):
                arrived((bsend.at[part], brecv.at[part]), sb.at[part])

        out = jax.ShapeDtypeStruct((layers, 2, rows, wide), BF16)
        anywhere = pl.BlockSpec(memory_space=pl.ANY)
        inside = pl.BlockSpec(memory_space=pltpu.VMEM)
        both = (out, out)
        operands = (gate_weight, up_weight, hidden_map.reshape(hrows, LANES), ffn_map.reshape(frows, LANES))
        grown = pl.pallas_call(
            kernel,
            out_shape=both,
            in_specs=[pl.BlockSpec(memory_space=pltpu.HBM)] * 4,
            out_specs=(inside, inside),
            scratch_shapes=[
                pltpu.VMEM(gate_weight.shape, BF16),
                pltpu.VMEM(gate_weight.shape, BF16),
                pltpu.VMEM((hrows, LANES), I32),
                pltpu.VMEM((frows, LANES), I32),
                pltpu.VMEM((2 * rows, lead), BF16),
                pltpu.VMEM((2 * rows, main), BF16),
                pltpu.VMEM((blocks, 2, lead), BF16),
                pltpu.VMEM((blocks, 2, lead), BF16),
                pltpu.VMEM((blocks, 2, main), BF16),
                pltpu.VMEM((blocks, 2, main), BF16),
                pltpu.VMEM((2 * rows, lead), BF16),
                pltpu.VMEM((splits, padded), I32),
                pltpu.VMEM((cols, narrow), BF16),
                pltpu.VMEM((cols, spread), BF16),
                pltpu.VMEM((2, splits, 2 * rows, LANES), BF16),
                pltpu.VMEM((2, splits, 2 * rows, LANES), BF16),
                pltpu.SemaphoreType.DMA((4,)),
                pltpu.SemaphoreType.DMA,
                pltpu.SemaphoreType.DMA,
                pltpu.SemaphoreType.DMA,
                pltpu.SemaphoreType.DMA,
                pltpu.SemaphoreType.DMA((2,)),
                pltpu.SemaphoreType.DMA((2,)),
                pltpu.SemaphoreType.REGULAR,
            ],
            compiler_params=pltpu.CompilerParams(collective_id=0, has_side_effects=True, vmem_limit_bytes=24 << 20),
            name="grow",
        )(*(pltpu.with_memory_space_constraint(x, pltpu.HBM) for x in operands))
        return pl.pallas_call(
            write_out,
            out_shape=both,
            in_specs=[inside] * 2,
            out_specs=(anywhere, anywhere),
            scratch_shapes=[pltpu.SemaphoreType.DMA((4,))],
            compiler_params=pltpu.CompilerParams(vmem_limit_bytes=24 << 20),
            name="write",
        )(*grown)

    weights = P(None, "section", "mp")
    out_specs = (P(None, None, "section", "mp"),) * 2
    return jax.shard_map(local, mesh=mesh, in_specs=(weights, weights, P(), P()), out_specs=out_specs, check_vma=False)
```

time: 41.4 us -> 37.1 us (0.90)
  local copies, waits for them, and re-layouts: 2.53 us -> 0 us
  Pallas kernels: 38.1 us -> 36.3 us
    unnamed x4 -> x0, local copies, waits for them, and re-layouts: 2.53 us -> none
    pallas_call x1 -> x2, Pallas kernels: 38.1 us -> 36.3 us  [the longest x1 35.4 us: local(): pl.pallas_call(kernel, out_shape=both, in_specs=[pl.BlockSpec(memory_spac...]
where the time goes in v2:
time: 37.1 us; the launch traced here: 37 us
  Pallas kernels  36.3 us (98%)
  between operations  0.64 us (2%)
    pallas_call x1, Pallas kernels, local(): pl.pallas_call(kernel, out_shape=both, in_specs=[pl.BlockSpec(memory_spac...  35.4 us
    pallas_call x1, Pallas kernels, local(): pl.pallas_call(write_out, out_shape=both, in_specs=[inside] * 2, out_spec...  0.89 us

profile of v2, /device:TPU:1, one launch (start us, length us, event | category | flops | bytes accessed | tf_op | source)
XLA Modules:
  0.0 37.0 jit_solution(8976223215380408711)
XLA Ops:
  0.6 35.4 %grow.1 = (bf16[2,2,32,1376]{3,2,1,0:T(8,128)(2,1)S(1)}, bf16[2,2,32,1376]{3,2,1,0:T(8,128)(2,1)S(1)}) custom-call(bf16[2,32,704]{2,1,0:T(8,128)(2,1)} %gate_h.1, bf16[2,32,704]{2,1,0:T(8,128)(2,1)} %up_h.1, s32[16,128]{1,0:T(8,128)} %bitcast.3, s32[42,128]{1,0:T(8,128)} %bitcast.2), custom_call_target="tpu_custom_call" | custom-call | tf_op jit(solution)/shard_map/grow/pallas_call | solution.py:241
  36.1 0.9 %write.1 = (bf16[2,2,32,1376]{3,2,1,0:T(8,128)(2,1)}, bf16[2,2,32,1376]{3,2,1,0:T(8,128)(2,1)}) custom-call(bf16[2,2,32,1376]{3,2,1,0:T(8,128)(2,1)S(1)} %get-tuple-element.4.gate_v, bf16[2,2,32,1376]{3,2,1,0:T(8,128)(2,1)S(1)} %get-tuple-element.5.up_v), custom_call_target="tpu_custom_call" | custom-call | tf_op jit(solution)/shard_map/write/pallas_call | solution.py:275

commit v3 on v2

--- a/solution.py
+++ b/solution.py
@@ -39,9 +39,10 @@
 
 def write_out(gate_v, up_v, gate_h, up_h, sems):
     copies = [
-        pltpu.make_async_copy(src.at[layer], dst.at[layer], sems.at[2 * n + layer])
+        pltpu.make_async_copy(src.at[layer, part], dst.at[layer, part], sems.at[4 * n + 2 * layer + part])
         for n, (src, dst) in enumerate(((gate_v, gate_h), (up_v, up_h)))
         for layer in range(2)
+        for part in range(2)
     ]
     for copy in copies:
         copy.start()
@@ -159,13 +160,18 @@
                 colpick[m * LANES + filled : (m + 1) * LANES, :] = jnp.zeros((LANES - filled, narrow), BF16)
 
             def exchange(part, values):
-                chosen = lax.dot_general(values, colpick[...], (((1,), (1,)), ((), ())), preferred_element_type=F32).astype(BF16)
-                for m in range(splits):
-                    bsend[part, m] = chosen[:, m * LANES : (m + 1) * LANES]
-                for to in fellow[1:]:
+                def choose(to):
+                    picks = colpick[pl.ds(pl.multiple_of(to * LANES, LANES), LANES), :]
+                    chosen = lax.dot_general(values, picks, (((1,), (1,)), ((), ())), preferred_element_type=F32)
+                    bsend[part, to] = chosen.astype(BF16)
+
+                for k in sorted(range(1, splits), key=lambda k: -min(k % 4, 4 - k % 4)):
+                    to = fellow[k]
+                    choose(to)
                     pltpu.make_async_remote_copy(
                         bsend.at[part, to], brecv.at[part, col], sb.at[part], rb.at[part], device_id={"mp": to}, device_id_type=MESH
                     ).start()
+                choose(col)
                 brecv[part, col] = bsend[part, col]
 
             def arrived(buffers, sem):
@@ -277,7 +283,7 @@
             out_shape=both,
             in_specs=[inside] * 2,
             out_specs=(anywhere, anywhere),
-            scratch_shapes=[pltpu.SemaphoreType.DMA((4,))],
+            scratch_shapes=[pltpu.SemaphoreType.DMA((8,))],
             compiler_params=pltpu.CompilerParams(vmem_limit_bytes=24 << 20),
             name="write",
         )(*grown)

time: 37.1 us -> 36.1 us (0.973)
  Pallas kernels: 36.3 us -> 35.3 us
    pallas_call x1, Pallas kernels: 35.4 us -> 34.4 us  [local(): pl.pallas_call(kernel, out_shape=both, in_specs=[pl.BlockSpec(memory_spac...]
where the time goes in v3:
time: 36.1 us; the launch traced here: 36 us
  Pallas kernels  35.3 us (98%)
  between operations  0.64 us (2%)
    pallas_call x1, Pallas kernels, local(): pl.pallas_call(kernel, out_shape=both, in_specs=[pl.BlockSpec(memory_spac...  34.4 us
    pallas_call x1, Pallas kernels, local(): pl.pallas_call(write_out, out_shape=both, in_specs=[inside] * 2, out_spec...  0.92 us

profile of v3, /device:TPU:1, one launch (start us, length us, event | category | flops | bytes accessed | tf_op | source)
XLA Modules:
  0.0 36.0 jit_solution(8179273731460614279)
XLA Ops:
  0.6 34.4 %grow.1 = (bf16[2,2,32,1376]{3,2,1,0:T(8,128)(2,1)S(1)}, bf16[2,2,32,1376]{3,2,1,0:T(8,128)(2,1)S(1)}) custom-call(bf16[2,32,704]{2,1,0:T(8,128)(2,1)} %gate_h.1, bf16[2,32,704]{2,1,0:T(8,128)(2,1)} %up_h.1, s32[16,128]{1,0:T(8,128)} %bitcast.3, s32[42,128]{1,0:T(8,128)} %bitcast.2), custom_call_target="tpu_custom_call" | custom-call | tf_op jit(solution)/shard_map/grow/pallas_call | solution.py:247
  35.0 0.9 %write.1 = (bf16[2,2,32,1376]{3,2,1,0:T(8,128)(2,1)}, bf16[2,2,32,1376]{3,2,1,0:T(8,128)(2,1)}) custom-call(bf16[2,2,32,1376]{3,2,1,0:T(8,128)(2,1)S(1)} %get-tuple-element.4.gate_v, bf16[2,2,32,1376]{3,2,1,0:T(8,128)(2,1)S(1)} %get-tuple-element.5.up_v), custom_call_target="tpu_custom_call" | custom-call | tf_op jit(solution)/shard_map/write/pallas_call | solution.py:281

commit v4 on v3

--- a/solution.py
+++ b/solution.py
@@ -89,7 +89,7 @@
             fellow = [jnp.where(col + k >= splits, col + k - splits, col + k) for k in range(splits)]
 
             barrier = pltpu.get_barrier_semaphore()
-            for d, q in near:
+            for d, q in sorted(near, key=lambda s: -(min(s[0], z_chips - s[0]) + 2 * (s[1] // 2))):
                 pl.semaphore_signal(barrier, 1, device_id={"section": seat[q] + ring[d]}, device_id_type=MESH)
             for to in fellow[1:]:
                 pl.semaphore_signal(barrier, 1, device_id={"mp": to}, device_id_type=MESH)
@@ -139,8 +139,15 @@
                     src.at[to], dst.at[me], ss, rs, device_id={"section": to}, device_id_type=MESH
                 ).start()
 
-            for d, q in near:
-                send(1, seat[q] + ring[d])
+            n_near = 2 * reach + 1
+            turned = jnp.where(z < reach, reach - z, jnp.where(z >= z_chips - reach, z_chips + reach - z, 0))
+            for i in range(n_near):
+                e = jnp.where(i + turned >= n_near, i + turned - n_near, i + turned)
+                ahead = z - reach + e
+                ahead = jnp.where(ahead < 0, ahead + z_chips, jnp.where(ahead >= z_chips, ahead - z_chips, ahead))
+                for q in range(1, 4):
+                    send(1, seat[q] + 2 * ahead)
+                pl.when(e != reach)(functools.partial(send, 1, seat[0] + 2 * ahead))
 
             loads[3].wait()
             for m in range(splits):

time: 36.1 us -> 36.1 us (level)
  no operation moved by 1% of the time
where the time goes in v4:
time: 36.1 us; the launch traced here: 35.9 us
  Pallas kernels  35.3 us (98%)
  between operations  0.64 us (2%)
    pallas_call x1, Pallas kernels, local(): pl.pallas_call(kernel, out_shape=both, in_specs=[pl.BlockSpec(memory_spac...  34.4 us
    pallas_call x1, Pallas kernels, local(): pl.pallas_call(write_out, out_shape=both, in_specs=[inside] * 2, out_spec...  0.92 us

profile of v4, /device:TPU:1, one launch (start us, length us, event | category | flops | bytes accessed | tf_op | source)
XLA Modules:
  0.0 35.9 jit_solution(1664609023965640732)
XLA Ops:
  0.6 34.4 %grow.1 = (bf16[2,2,32,1376]{3,2,1,0:T(8,128)(2,1)S(1)}, bf16[2,2,32,1376]{3,2,1,0:T(8,128)(2,1)S(1)}) custom-call(bf16[2,32,704]{2,1,0:T(8,128)(2,1)} %gate_h.1, bf16[2,32,704]{2,1,0:T(8,128)(2,1)} %up_h.1, s32[16,128]{1,0:T(8,128)} %bitcast.3, s32[42,128]{1,0:T(8,128)} %bitcast.2), custom_call_target="tpu_custom_call" | custom-call | tf_op jit(solution)/shard_map/grow/pallas_call | solution.py:254
  35.0 0.9 %write.1 = (bf16[2,2,32,1376]{3,2,1,0:T(8,128)(2,1)}, bf16[2,2,32,1376]{3,2,1,0:T(8,128)(2,1)}) custom-call(bf16[2,2,32,1376]{3,2,1,0:T(8,128)(2,1)S(1)} %get-tuple-element.4.gate_v, bf16[2,2,32,1376]{3,2,1,0:T(8,128)(2,1)S(1)} %get-tuple-element.5.up_v), custom_call_target="tpu_custom_call" | custom-call | tf_op jit(solution)/shard_map/write/pallas_call | solution.py:288

commit v5 on v3

--- a/solution.py
+++ b/solution.py
@@ -169,7 +169,7 @@
                     to = fellow[k]
                     choose(to)
                     pltpu.make_async_remote_copy(
-                        bsend.at[part, to], brecv.at[part, col], sb.at[part], rb.at[part], device_id={"mp": to}, device_id_type=MESH
+                        bsend.at[part, to], brecv.at[part, col], sb.at[part], rb.at[part, col], device_id={"mp": to}, device_id_type=MESH
                     ).start()
                 choose(col)
                 brecv[part, col] = bsend[part, col]
@@ -179,10 +179,13 @@
                 pltpu.make_async_copy(src.at[pl.ds(0, dst.shape[0] - 1)], dst.at[pl.ds(0, dst.shape[0] - 1)], sem).wait()
 
             def grow(part, last):
-                arrived((bsend.at[part], brecv.at[part]), rb.at[part])
                 added = jnp.zeros((2 * rows, spread), F32)
-                for m in range(splits):
-                    added += jnp.dot(brecv[part, m], place[m * LANES : (m + 1) * LANES, :], preferred_element_type=F32)
+                for k in sorted(range(splits), key=lambda k: min(k % 4, 4 - k % 4) + k // 4):
+                    m = fellow[k]
+                    if k:
+                        pltpu.make_async_copy(bsend.at[part, m], brecv.at[part, m], rb.at[part, m]).wait()
+                    spots = place[pl.ds(pl.multiple_of(m * LANES, LANES), LANES), :]
+                    added += jnp.dot(brecv[part, m], spots, preferred_element_type=F32)
                 first_half = lane_iota((2 * rows, LANES)) < tail
                 for layer, end in enumerate((pltpu.roll(last, LANES - tail, 1), last)):
                     head = (added[:, :LANES] + jnp.where(first_half, end, 0.0)).astype(BF16)
@@ -272,7 +275,7 @@
                 pltpu.SemaphoreType.DMA,
                 pltpu.SemaphoreType.DMA,
                 pltpu.SemaphoreType.DMA((2,)),
-                pltpu.SemaphoreType.DMA((2,)),
+                pltpu.SemaphoreType.DMA((2, splits)),
                 pltpu.SemaphoreType.REGULAR,
             ],
             compiler_params=pltpu.CompilerParams(collective_id=0, has_side_effects=True, vmem_limit_bytes=24 << 20),

time: 36.1 us -> 36.1 us (level)
  no operation moved by 1% of the time
where the time goes in v5:
time: 36.1 us; the launch traced here: 35.9 us
  Pallas kernels  35.3 us (98%)
  between operations  0.64 us (2%)
    pallas_call x1, Pallas kernels, local(): pl.pallas_call(kernel, out_shape=both, in_specs=[pl.BlockSpec(memory_spac...  34.3 us
    pallas_call x1, Pallas kernels, local(): pl.pallas_call(write_out, out_shape=both, in_specs=[inside] * 2, out_spec...  0.92 us

profile of v5, /device:TPU:1, one launch (start us, length us, event | category | flops | bytes accessed | tf_op | source)
XLA Modules:
  0.0 35.9 jit_solution(6567176873027604470)
XLA Ops:
  0.6 34.3 %grow.1 = (bf16[2,2,32,1376]{3,2,1,0:T(8,128)(2,1)S(1)}, bf16[2,2,32,1376]{3,2,1,0:T(8,128)(2,1)S(1)}) custom-call(bf16[2,32,704]{2,1,0:T(8,128)(2,1)} %gate_h.1, bf16[2,32,704]{2,1,0:T(8,128)(2,1)} %up_h.1, s32[16,128]{1,0:T(8,128)} %bitcast.3, s32[42,128]{1,0:T(8,128)} %bitcast.2), custom_call_target="tpu_custom_call" | custom-call | tf_op jit(solution)/shard_map/grow/pallas_call | solution.py:250
  35.0 0.9 %write.1 = (bf16[2,2,32,1376]{3,2,1,0:T(8,128)(2,1)}, bf16[2,2,32,1376]{3,2,1,0:T(8,128)(2,1)}) custom-call(bf16[2,2,32,1376]{3,2,1,0:T(8,128)(2,1)S(1)} %get-tuple-element.4.gate_v, bf16[2,2,32,1376]{3,2,1,0:T(8,128)(2,1)S(1)} %get-tuple-element.5.up_v), custom_call_target="tpu_custom_call" | custom-call | tf_op jit(solution)/shard_map/write/pallas_call | solution.py:284
